TPU v7x, 32 devices: a whole 2x2x4 slice. The times are simulated.
32 devices in a mesh: gx: 4 (over x, core), gy: 4 (over z), gz: 2 (over y).
Axes of the slice: x: 2, y: 2, z: 4, core: 2. Of those that a mesh axis runs over, the one named last changes fastest.
Arguments:
- embeds: bfloat16 [256, 128, 2048], P(('gx', 'gy', 'gz')), may hold values from -6 to 6
- dest_device: int32 [256], P(('gx', 'gy', 'gz')), may hold values from 0 to 31, as said below
- shuffle_key: int32 [256], P(('gx', 'gy', 'gz')), may hold values from 0 to 255, each once
- lengths: int32 [8], replicated, may hold values from 1 to 4096
- gain: float32 [2048], replicated, may hold values from 0.1 to 1.9
Outputs:
- packed: bfloat16 [512, 128, 2048], P(('gx', 'gy', 'gz'))
Inputs may be any that keep to these rules, and one draw needn't show every extreme that they name: `dest_device`: device numbers are ((gx * 4) + gy) * 2 + gz. A device receives at most 16 tiles, and in every draw some devices receive exactly 16. The 2 devices sharing gx and gy send at most one tile to any one device and exactly 8 tiles to the devices of each gz index. Of one device's tiles at most 4 go to devices of one gz index, and some device reaches that.
All inputs are finite; a program needn't handle non-finite values.
Results may differ from a plain program's by a relative error of at most 0.001.
Values may be sent and summed in bfloat16 or wider, within the bound.
A program may use at most 128 MiB of HBM per device.

v0:
```python
import jax
import jax.numpy as jnp
from jax import lax
from jax.sharding import PartitionSpec as P

TILES_SEQ = 32


def normalize(rows, tile_ids, lengths, gain):
    rows_tile = rows.shape[1]
    values = rows.astype(jnp.float32)
    meansq = jnp.mean(values * values, axis=-1, keepdims=True)
    scaled = values * lax.rsqrt(jnp.maximum(meansq, 0.25)) * gain
    seq_ids = tile_ids // TILES_SEQ
    match = seq_ids[:, None] == jnp.arange(lengths.shape[0], dtype=jnp.int32)[None, :]
    limit = jnp.sum(jnp.where(match, lengths[None, :], 0), axis=1)
    position = (tile_ids % TILES_SEQ)[:, None] * rows_tile + jnp.arange(rows_tile, dtype=jnp.int32)[
        None, :
    ]
    keep = position < limit[:, None]
    return jnp.where(keep[:, :, None], scaled, 0.0).astype(jnp.bfloat16)


def place(table, rows, numbers):
    moved = jnp.einsum(
        "sk,krd->srd", table.astype(jnp.bfloat16), rows, preferred_element_type=jnp.float32
    ).astype(jnp.bfloat16)
    picked = tuple(
        (
            jnp.sum(jnp.where(table, values[None, :] + 1, 0), axis=1).astype(jnp.int32) - 1
            for values in numbers
        )
    )
    return (moved, picked)


def shards(embeds, dest_device, shuffle_key, lengths, gain):
    tiles_here = embeds.shape[0]
    depth_count = lax.axis_size("gz")
    group_count = lax.axis_size("gx") * lax.axis_size("gy")
    device_index = (
        lax.axis_index("gx") * lax.axis_size("gy") + lax.axis_index("gy")
    ) * depth_count + lax.axis_index("gz")
    tile_ids = device_index * tiles_here + jnp.arange(tiles_here, dtype=jnp.int32)
    payload = normalize(embeds, tile_ids, lengths, gain)
    per_peer = (tiles_here + depth_count - 1) // depth_count
    first_slots = (
        dest_device % depth_count * per_peer
        + jnp.arange(tiles_here, dtype=jnp.int32) // depth_count
    )
    first_table = (
        jnp.arange(depth_count * per_peer, dtype=jnp.int32)[:, None] == first_slots[None, :]
    )
    first_rows, first_numbers = place(first_table, payload, (dest_device, shuffle_key, tile_ids))
    arrived_rows, arrived_dests, arrived_keys, arrived_ids = (
        lax.all_to_all(first_rows, "gz", split_axis=0, concat_axis=0, tiled=True),
        lax.all_to_all(first_numbers[0], "gz", split_axis=0, concat_axis=0, tiled=True),
        lax.all_to_all(first_numbers[1], "gz", split_axis=0, concat_axis=0, tiled=True),
        lax.all_to_all(first_numbers[2], "gz", split_axis=0, concat_axis=0, tiled=True),
    )
    second_slots = jnp.where(arrived_dests >= 0, arrived_dests // depth_count, -1)
    second_table = jnp.arange(group_count, dtype=jnp.int32)[:, None] == second_slots[None, :]
    second_rows, second_numbers = place(
        second_table, arrived_rows, (arrived_dests, arrived_keys, arrived_ids)
    )
    final_rows, final_dests, final_keys, final_ids = (
        lax.all_to_all(second_rows, ("gx", "gy"), split_axis=0, concat_axis=0, tiled=True),
        lax.all_to_all(second_numbers[0], ("gx", "gy"), split_axis=0, concat_axis=0, tiled=True),
        lax.all_to_all(second_numbers[1], ("gx", "gy"), split_axis=0, concat_axis=0, tiled=True),
        lax.all_to_all(second_numbers[2], ("gx", "gy"), split_axis=0, concat_axis=0, tiled=True),
    )
    valid = final_dests >= 0
    earlier = valid[None, :] & valid[:, None] & (final_keys[None, :] < final_keys[:, None])
    rank = jnp.sum(earlier.astype(jnp.int32), axis=1)
    final_slots = jnp.where(valid, rank, -1)
    final_table = jnp.arange(2 * tiles_here, dtype=jnp.int32)[:, None] == final_slots[None, :]
    packed_rows, packed_numbers = place(final_table, final_rows, (final_ids,))
    return packed_rows


def solution(mesh):
    return jax.shard_map(
        shards,
        mesh=mesh,
        in_specs=(
            P(("gx", "gy", "gz"), None, None),
            P(("gx", "gy", "gz")),
            P(("gx", "gy", "gz")),
            P(),
            P(),
        ),
        out_specs=P(("gx", "gy", "gz"), None, None),
        check_vma=False,
    )
```

profile of v0, /device:TPU:9, one launch (start us, length us, event | category | flops | bytes accessed | tf_op | source)
XLA Modules:
  0.0 331.2 jit_solution(3925120589455384015)
XLA Ops:
  0.0 0.7 broadcast_add_fusion.3
  0.7 0.7 broadcast_add_fusion.2
  1.3 0.1 select_reduce_fusion.2
  1.5 0.7 sub.32
  2.1 3.1 all-to-all-start
  5.3 0.7 sub.37
  6.0 3.1 fusion
  9.1 0.8 select_reduce_fusion
  10.0 4.3 %fusion.3 = bf16[8,128,2048]{2,1,0:T(8,128)(2,1)} fusion(bf16[8,128,2048]{2,1,0:T(8,128)(2,1)} %param.5, f32[2048]{0:T(1024)} %param.9, f32[8,128]{1,0:T(8,128)S(1)} %maximum_rsqrt_fusion, pred[8,128]{1,0:T(8,128)(4,1)S(1)} %add_compare_fusion), kind=kLoop, calls=%fused_computation.5 | loop fusion | flops 10485760 | bytes 8401920 | tf_op jit(solution)/shard_map/convert_element_type | solution.py:21
  14.3 3.2 all-to-all-start.2
  17.5 0.5 broadcast.289
  18.0 0.6 reduce.10
  18.6 0.1 all_to_all.25
  18.7 1.4 all-to-all-done.2
  20.3 0.1 select_reduce_fusion.1
  20.4 0.7 copy.34
  21.0 7.6 %all-to-all-start.3 = ((s32[16,1,1]{2,1,0:T(1,128)}), s32[16,1,1]{2,1,0:T(1,128)S(1)}, u32[]{:S(2)}, u32[]{:S(2)}) async-start(s32[16,1,1]{2,1,0:T(1,128)} %copy.34), calls=%async_computation.3 | async-start | bytes 16384 | tf_op jit(solution)/shard_map/all_to_all | solution.py:69
  28.6 5.1 %fusion.12 = bf16[8,128,2048]{2,0,1:T(8,128)(2,1)S(1)} fusion(bf16[8,128,2048]{2,1,0:T(8,128)(2,1)} %fusion.3, s32[8]{0:T(128)S(1)} %get-tuple-element.12), kind=kOutput, calls=%fused_computation.13 | convolution fusion | flops 35651648 | bytes 8388640 | tf_op jit(solution)/shard_map/sk,krd->srd/dot_general | solution.py:25
  33.7 4.3 %copy.36 = bf16[8,128,2048]{2,1,0:T(8,128)(2,1)} copy(bf16[8,128,2048]{2,0,1:T(8,128)(2,1)S(1)} %fusion.12) | data formatting | bytes 8388608 | tf_op jit(solution)/shard_map/convert_element_type | solution.py:27
  38.0 5.6 %all-to-all-start.4 = ((bf16[8,128,2048]{2,1,0:T(8,128)(2,1)}), bf16[8,128,2048]{2,1,0:T(8,128)(2,1)}, u32[]{:S(2)}, u32[]{:S(2)}) async-start(bf16[8,128,2048]{2,1,0:T(8,128)(2,1)} %copy.36), calls=%async_computation.4 | async-start | bytes 8388608 | tf_op jit(solution)/shard_map/all_to_all | solution.py:56
  43.7 0.7 copy.32
  44.3 46.4 %all-to-all-done.4 = bf16[8,128,2048]{2,1,0:T(8,128)(2,1)} async-done(((bf16[8,128,2048]{2,1,0:T(8,128)(2,1)}), bf16[8,128,2048]{2,1,0:T(8,128)(2,1)}, u32[]{:S(2)}, u32[]{:S(2)}) %all-to-all-start.4) | async-done | bytes 4194336 | tf_op jit(solution)/shard_map/all_to_all | solution.py:56
  90.7 6.9 %all-to-all-start.1 = ((s32[16,1,1]{2,1,0:T(1,128)}), s32[16,1,1]{2,1,0:T(1,128)S(1)}, u32[]{:S(2)}, u32[]{:S(2)}) async-start(s32[16,1,1]{2,1,0:T(1,128)} %copy.32), calls=%async_computation.1 | async-start | bytes 16384 | tf_op jit(solution)/shard_map/all_to_all | solution.py:68
  97.6 8.2 %convolution_convert_fusion = bf16[16,128,2048]{2,0,1:T(8,128)(2,1)} fusion(bf16[8,128,2048]{2,1,0:T(8,128)(2,1)} %all-to-all-done.4, s32[8]{0:T(128)S(1)} %get-tuple-element.10), kind=kOutput, calls=%fused_computation.9 | convolution fusion | flops 71303296 | bytes 12582944 | tf_op jit(solution)/shard_map/sk,krd->srd/dot_general | solution.py:25
  105.8 11.2 %copy.38 = bf16[16,128,2048]{2,1,0:T(8,128)(2,1)} copy(bf16[16,128,2048]{2,0,1:T(8,128)(2,1)} %convolution_convert_fusion) | data formatting | bytes 16777216 | tf_op jit(solution)/shard_map/convert_element_type | solution.py:27
  117.0 6.0 %all-to-all-start.5 = ((bf16[16,128,2048]{2,1,0:T(8,128)(2,1)}), bf16[16,128,2048]{2,1,0:T(8,128)(2,1)}, u32[]{:S(2)}, u32[]{:S(2)}) async-start(bf16[16,128,2048]{2,1,0:T(8,128)(2,1)} %copy.38), calls=%async_computation.5 | async-start | bytes 16777216 | tf_op jit(solution)/shard_map/all_to_all | solution.py:67
  123.1 0.4 reduce.3
  123.4 0.4 compare_reduce_fusion
  123.8 0.2 convert_reduce_fusion
  124.0 179.4 %all-to-all-done.5 = bf16[16,128,2048]{2,1,0:T(8,128)(2,1)} async-done(((bf16[16,128,2048]{2,1,0:T(8,128)(2,1)}), bf16[16,128,2048]{2,1,0:T(8,128)(2,1)}, u32[]{:S(2)}, u32[]{:S(2)}) %all-to-all-start.5) | async-done | bytes 8388640 | tf_op jit(solution)/shard_map/all_to_all | solution.py:67
  303.5 16.1 %fusion.6 = bf16[16,128,2048]{2,0,1:T(8,128)(2,1)} fusion(bf16[16,128,2048]{2,1,0:T(8,128)(2,1)} %all-to-all-done.5, s32[16]{0:T(128)S(1)} %broadcast_select_fusion), kind=kOutput, calls=%fused_computation.8 | convolution fusion | flops 138412288 | bytes 16777280 | tf_op jit(solution)/shard_map/sk,krd->srd/dot_general | solution.py:25
  319.6 11.7 %copy.40 = bf16[16,128,2048]{2,1,0:T(8,128)(2,1)} copy(bf16[16,128,2048]{2,0,1:T(8,128)(2,1)} %fusion.6) | data formatting | bytes 16777216 | tf_op jit(solution)/shard_map/convert_element_type | solution.py:27
  (13 shorter events, 0.2 us)
Async XLA Ops:
  2.1 12.2 %all-to-all-start = ((s32[2,4,1]{1,2,0:T(1,128)}), s32[2,4,1]{1,2,0:T(1,128)S(1)}, u32[]{:S(2)}, u32[]{:S(2)}) async-start(s32[2,4,1]{1,2,0:T(1,128)} %bitcast), calls=%async_computation | async-start | bytes 2048 | tf_op jit(solution)/shard_map/all_to_all | solution.py:57
  14.3 5.8 %all-to-all-start.2 = ((s32[2,4,1]{1,2,0:T(1,128)}), s32[2,4,1]{1,2,0:T(1,128)S(1)}, u32[]{:S(2)}, u32[]{:S(2)}) async-start(s32[2,4,1]{1,2,0:T(1,128)} %bitcast.2), calls=%async_computation.2 | async-start | bytes 2048 | tf_op jit(solution)/shard_map/all_to_all | solution.py:58
  21.0 17.0 %all-to-all-start.3 = ((s32[16,1,1]{2,1,0:T(1,128)}), s32[16,1,1]{2,1,0:T(1,128)S(1)}, u32[]{:S(2)}, u32[]{:S(2)}) async-start(s32[16,1,1]{2,1,0:T(1,128)} %copy.34), calls=%async_computation.3 | async-start | bytes 16384 | tf_op jit(solution)/shard_map/all_to_all | solution.py:69
  38.0 52.7 %all-to-all-start.4 = ((bf16[8,128,2048]{2,1,0:T(8,128)(2,1)}), bf16[8,128,2048]{2,1,0:T(8,128)(2,1)}, u32[]{:S(2)}, u32[]{:S(2)}) async-start(bf16[8,128,2048]{2,1,0:T(8,128)(2,1)} %copy.36), calls=%async_computation.4 | async-start | bytes 8388608 | tf_op jit(solution)/shard_map/all_to_all | solution.py:56
  90.7 26.3 %all-to-all-start.1 = ((s32[16,1,1]{2,1,0:T(1,128)}), s32[16,1,1]{2,1,0:T(1,128)S(1)}, u32[]{:S(2)}, u32[]{:S(2)}) async-start(s32[16,1,1]{2,1,0:T(1,128)} %copy.32), calls=%async_computation.1 | async-start | bytes 16384 | tf_op jit(solution)/shard_map/all_to_all | solution.py:68
  117.0 186.4 %all-to-all-start.5 = ((bf16[16,128,2048]{2,1,0:T(8,128)(2,1)}), bf16[16,128,2048]{2,1,0:T(8,128)(2,1)}, u32[]{:S(2)}, u32[]{:S(2)}) async-start(bf16[16,128,2048]{2,1,0:T(8,128)(2,1)} %copy.38), calls=%async_computation.5 | async-start | bytes 16777216 | tf_op jit(solution)/shard_map/all_to_all | solution.py:67
where the time goes:
time: 337 us; the launch traced here: 331 us
  waiting for transfers between devices  227 us (67%)
  starting transfers between devices  32.5 us (10%)
  local copies, waits for them, and re-layouts  30.6 us (9%)
  matrix products  29.4 us (9%)
  other arithmetic  11.5 us (3%)
    all_to_all x1, waiting for transfers between devices, shards(): lax.all_to_all(second_rows, ('gx', 'gy'), split_axis=0, concat_axis=0, ti...  179 us
    all_to_all x1, waiting for transfers between devices, shards(): lax.all_to_all(first_rows, 'gz', split_axis=0, concat_axis=0, tiled=True)  46.4 us
    dot_general x3, matrix products, place(): jnp.einsum('sk,krd->srd', table.astype(jnp.bfloat16), rows, preferred_ele...  29.4 us
    convert_element_type x3, local copies, waits for them, and re-layouts, place(): moved = jnp.einsum('sk,krd->srd', table.astype(jnp.bfloat16), rows, prefe...  27.2 us
    all_to_all x1, starting transfers between devices, shards(): lax.all_to_all(second_numbers[1], ('gx', 'gy'), split_axis=0, concat_axis...  7.6 us
    all_to_all x1, starting transfers between devices, shards(): lax.all_to_all(second_numbers[0], ('gx', 'gy'), split_axis=0, concat_axis...  6.88 us
  transfers between devices with their start and end apart: 6, of which 3 were waited for; matrix products, arithmetic and copies ran while one was open for 12% of the time, Pallas kernels for 0%

commit v1 on v0

v1 whole, which is shorter than its diff:
```python
import functools

import jax
import jax.numpy as jnp
from jax import lax
from jax.experimental import pallas as pl
from jax.experimental.pallas import tpu as pltpu
from jax.sharding import PartitionSpec as P

TILES_SEQ = 32
MESH = pl.DeviceIdType.MESH


def exchange_kernel(
    sizes, first_ref, limit_ref, second_ref, x_ref, gain_ref, recv_ref,
    first, outgoing, y_send, y_recv, g_send, g_recv, own_sem, *arrived,
):
    nx, ny, depth, per_peer, chunks, rows = sizes
    groups = nx * ny
    gx, gy, gz = lax.axis_index("gx"), lax.axis_index("gy"), lax.axis_index("gz")
    group = gx * ny + gy
    offsets = [(dx, dy) for dy in sorted(range(ny), key=lambda d: abs(d - ny // 2)) for dx in range(nx)]
    offsets.remove((0, 0))

    def normed(c, slot):
        tile = first_ref[slot]
        values = x_ref[tile, pl.ds(c * rows, rows), :].astype(jnp.float32)
        meansq = jnp.mean(values * values, axis=-1, keepdims=True)
        scaled = values * lax.rsqrt(jnp.maximum(meansq, 0.25)) * gain_ref[...]
        row = c * rows + lax.broadcasted_iota(jnp.int32, (rows, 1), 0)
        return jnp.where(row < limit_ref[slot], scaled, 0.0).astype(jnp.bfloat16)

    def y_copy(c, dz):
        peer = lax.rem(gz + dz, depth)
        return pltpu.make_async_remote_copy(
            src_ref=first.at[c, dz - 1],
            dst_ref=arrived[c].at[pl.ds(gz * per_peer, per_peer)],
            send_sem=y_send.at[c, dz - 1],
            recv_sem=y_recv.at[c, dz - 1],
            device_id=(gx, gy, peer),
            device_id_type=MESH,
        )

    def y_wait(c, dz):
        origin = lax.rem(gz + depth - dz, depth)
        pltpu.make_async_remote_copy(
            src_ref=first.at[c, dz - 1],
            dst_ref=arrived[c].at[pl.ds(origin * per_peer, per_peer)],
            send_sem=y_send.at[c, dz - 1],
            recv_sem=y_recv.at[c, dz - 1],
            device_id=(gx, gy, origin),
            device_id_type=MESH,
        ).wait_recv()

    def peer_of(k):
        dx, dy = offsets[k]
        return lax.rem(gx + dx, nx), lax.rem(gy + dy, ny)

    def g_copy(c, k):
        px, py = peer_of(k)
        return pltpu.make_async_remote_copy(
            src_ref=outgoing.at[c, k],
            dst_ref=recv_ref.at[c, group],
            send_sem=g_send.at[c, k],
            recv_sem=g_recv.at[c, k],
            device_id=(px, py, gz),
            device_id_type=MESH,
        )

    def own_copy(c):
        return pltpu.make_async_copy(outgoing.at[c, groups - 1], recv_ref.at[c, group], own_sem.at[c])

    def prepare(c):
        for dz in range(1, depth):
            peer = lax.rem(gz + dz, depth)
            for p in range(per_peer):
                first[c, dz - 1, p] = normed(c, peer * per_peer + p)
        for p in range(per_peer):
            arrived[c][gz * per_peer + p] = normed(c, gz * per_peer + p)
        for dz in range(1, depth):
            y_copy(c, dz).start()

    def forward(c):
        for dz in range(1, depth):
            y_wait(c, dz)
        for k in range(groups - 1):
            px, py = peer_of(k)
            outgoing[c, k] = arrived[c][second_ref[px * ny + py]]
        outgoing[c, groups - 1] = arrived[c][second_ref[group]]
        for k in range(groups - 1):
            g_copy(c, k).start()
        own_copy(c).start()

    lead = min(2, chunks)
    for c in range(lead):
        prepare(c)

    for c in range(chunks - lead):
        forward(c)
        prepare(c + lead)

    for c in range(chunks - lead, chunks):
        forward(c)

    for c in range(chunks):
        for dz in range(1, depth):
            y_copy(c, dz).wait_send()

    @pl.loop(0, chunks)
    def _(c):
        for k in range(groups - 1):
            copy = g_copy(c, k)
            copy.wait_send()
            dx, dy = offsets[k]
            sx, sy = lax.rem(gx + nx - dx, nx), lax.rem(gy + ny - dy, ny)
            pltpu.make_async_remote_copy(
                src_ref=outgoing.at[c, k],
                dst_ref=recv_ref.at[c, sx * ny + sy],
                send_sem=g_send.at[c, k],
                recv_sem=g_recv.at[c, k],
                device_id=(sx, sy, gz),
                device_id_type=MESH,
            ).wait_recv()
        own_copy(c).wait()


def place_kernel(source_ref, filled_ref, block_ref, out_ref):
    chunks, _, rows, _ = block_ref.shape
    slot = pl.program_id(0)

    @pl.when(filled_ref[slot] == 1)
    def _():
        for c in range(chunks):
            out_ref[0, pl.ds(c * rows, rows), :] = block_ref[c, 0]

    @pl.when(filled_ref[slot] == 0)
    def _():
        out_ref[...] = jnp.zeros_like(out_ref)


def shards(embeds, dest_device, shuffle_key, lengths, gain):
    tiles_here, tile_rows, width = embeds.shape
    nx, ny, depth = lax.axis_size("gx"), lax.axis_size("gy"), lax.axis_size("gz")
    groups = nx * ny
    group = lax.axis_index("gx") * ny + lax.axis_index("gy")
    gz = lax.axis_index("gz")
    me = group * depth + gz
    per_peer = (tiles_here + depth - 1) // depth
    slots = depth * per_peer
    chunks = 8 if tile_rows % 128 == 0 else 1
    rows = tile_rows // chunks

    both = lax.all_gather(
        jnp.stack([dest_device, shuffle_key]), ("gx", "gy", "gz"), axis=0, tiled=False
    )
    dests = both[:, 0, :]
    keys = both[:, 1, :]
    depths = dests % depth
    order = jnp.arange(tiles_here, dtype=jnp.int32)
    before = (depths[:, None, :] == depths[:, :, None]) & (order[None, None, :] < order[None, :, None])
    spot = jnp.sum(before.astype(jnp.int32), axis=2)

    here_dest = lax.dynamic_slice_in_dim(dests, me, 1, 0)[0]
    here_spot = lax.dynamic_slice_in_dim(spot, me, 1, 0)[0]
    here_slot = here_dest % depth * per_peer + here_spot
    hit = here_slot[None, :] == jnp.arange(slots, dtype=jnp.int32)[:, None]
    first = jnp.sum(jnp.where(hit, order[None, :], 0), axis=1).astype(jnp.int32)
    tile_ids = me * tiles_here + order
    match = (tile_ids // TILES_SEQ)[:, None] == jnp.arange(lengths.shape[0], dtype=jnp.int32)[None, :]
    limit = jnp.sum(jnp.where(match, lengths[None, :], 0), axis=1) - tile_ids % TILES_SEQ * tile_rows
    limits = jnp.sum(jnp.where(hit, jnp.maximum(limit, 0)[None, :], 0), axis=1).astype(jnp.int32)

    by_group_dest = dests.reshape(groups, depth * tiles_here)
    by_group_key = keys.reshape(groups, depth * tiles_here)
    pair_dest = lax.dynamic_slice_in_dim(by_group_dest, group, 1, 0)[0]
    pair_spot = lax.dynamic_slice_in_dim(spot.reshape(groups, depth * tiles_here), group, 1, 0)[0]
    pair_slot = jnp.arange(depth * tiles_here, dtype=jnp.int32) // tiles_here * per_peer + pair_spot
    wanted = jnp.arange(groups, dtype=jnp.int32) * depth + gz
    second = jnp.sum(
        jnp.where(pair_dest[None, :] == wanted[:, None], pair_slot[None, :], 0), axis=1
    ).astype(jnp.int32)

    mine = by_group_dest == me
    key_of = jnp.sum(jnp.where(mine, by_group_key + 1, 0), axis=1)
    valid = key_of > 0
    rank = jnp.sum((valid[None, :] & (key_of[None, :] < key_of[:, None])).astype(jnp.int32), axis=1)
    cap = 2 * tiles_here
    at = valid[None, :] & (rank[None, :] == jnp.arange(cap, dtype=jnp.int32)[:, None])
    source = jnp.sum(jnp.where(at, jnp.arange(groups, dtype=jnp.int32)[None, :], 0), axis=1).astype(jnp.int32)
    filled = jnp.sum(at.astype(jnp.int32), axis=1).astype(jnp.int32)

    smem = pl.BlockSpec(memory_space=pltpu.SMEM)
    vmem = pl.BlockSpec(memory_space=pltpu.VMEM)
    sent = chunks * groups * rows * width * 2
    received = pl.pallas_call(
        functools.partial(exchange_kernel, (nx, ny, depth, per_peer, chunks, rows)),
        out_shape=jax.ShapeDtypeStruct((chunks, groups, rows, width), jnp.bfloat16),
        in_specs=[smem, smem, smem, vmem, vmem],
        out_specs=pl.BlockSpec(memory_space=pl.ANY),
        scratch_shapes=[
            pltpu.VMEM((chunks, depth - 1, per_peer, rows, width), jnp.bfloat16),
            pltpu.VMEM((chunks, groups, rows, width), jnp.bfloat16),
            pltpu.SemaphoreType.DMA((chunks, depth - 1)),
            pltpu.SemaphoreType.DMA((chunks, depth - 1)),
            pltpu.SemaphoreType.DMA((chunks, groups)),
            pltpu.SemaphoreType.DMA((chunks, groups)),
            pltpu.SemaphoreType.DMA((chunks,)),
        ]
        + [pltpu.VMEM((slots, rows, width), jnp.bfloat16)] * chunks,
        compiler_params=pltpu.CompilerParams(
            has_side_effects=True, vmem_limit_bytes=52 * 1024 * 1024
        ),
        name="exchange",
    )(first, limits, second, embeds, gain.reshape(1, width))

    return pl.pallas_call(
        place_kernel,
        grid_spec=pltpu.PrefetchScalarGridSpec(
            num_scalar_prefetch=2,
            grid=(cap,),
            in_specs=[
                pl.BlockSpec((chunks, 1, rows, width), lambda s, source, filled: (0, source[s], 0, 0))
            ],
            out_specs=pl.BlockSpec((1, tile_rows, width), lambda s, source, filled: (s, 0, 0)),
        ),
        out_shape=jax.ShapeDtypeStruct((cap, tile_rows, width), jnp.bfloat16),
        name="place",
    )(source, filled, received)


def solution(mesh):
    return jax.shard_map(
        shards,
        mesh=mesh,
        in_specs=(
            P(("gx", "gy", "gz"), None, None),
            P(("gx", "gy", "gz")),
            P(("gx", "gy", "gz")),
            P(),
            P(),
        ),
        out_specs=P(("gx", "gy", "gz"), None, None),
        check_vma=False,
    )
```

time: 337 us -> 282 us (0.84); the launches traced: 331 us -> 281 us
  waiting for transfers between devices: 227 us -> 0 us
  Pallas kernels: 0 us -> 218 us
  blocking collectives: 0 us -> 58 us
  starting transfers between devices: 32.5 us -> 0 us
  matrix products: 29.4 us -> 0 us
  local copies, waits for them, and re-layouts: 30.6 us -> 1.21 us
  other arithmetic: 11.5 us -> 3.82 us
    all_to_all x6 -> x0, waiting for transfers between devices: 227 us -> none  [the longest x1 179 us: shards(): lax.all_to_all(second_rows, ('gx', 'gy'), split_axis=0, concat_axis=0, ti...]
    pallas_call x0 -> x2, Pallas kernels: none -> 218 us  [the longest x1 207 us: shards(): pl.pallas_call(functools.partial(exchange_kernel, (nx, ny, depth, per_pee...]
    all_gather x0 -> x1, blocking collectives: none -> 58 us  [shards(): lax.all_gather(jnp.stack([dest_device, shuffle_key]), ('gx', 'gy', 'gz'),...]
    all_to_all x6 -> x0, starting transfers between devices: 32.5 us -> none  [the longest x1 7.6 us: shards(): lax.all_to_all(second_numbers[1], ('gx', 'gy'), split_axis=0, concat_axis...]
    dot_general x3 -> x0, matrix products: 29.4 us -> none  [place(): jnp.einsum('sk,krd->srd', table.astype(jnp.bfloat16), rows, preferred_ele...]
    convert_element_type x3 -> x0, local copies, waits for them, and re-layouts: 27.2 us -> none  [place(): moved = jnp.einsum('sk,krd->srd', table.astype(jnp.bfloat16), rows, prefe...]
    convert_element_type x1 -> x0, other arithmetic: 4.33 us -> none  [normalize(): return jnp.where(keep[:, :, None], scaled, 0.0).astype(jnp.bfloat16)]
  transfers between devices with their start and end apart: 6 -> 0, of which waited for: 3 -> 0; matrix products, arithmetic and copies ran while one was open for 12% -> 0% of each run, Pallas kernels for 0% -> 0%
where the time goes in v1:
time: 282 us; the launch traced here: 281 us
  Pallas kernels  218 us (77%)
  blocking collectives  58 us (21%)
  other arithmetic  3.82 us (1%)
    pallas_call x1, Pallas kernels, shards(): pl.pallas_call(functools.partial(exchange_kernel, (nx, ny, depth, per_pee...  207 us
    all_gather x1, blocking collectives, shards(): lax.all_gather(jnp.stack([dest_device, shuffle_key]), ('gx', 'gy', 'gz'),...  58 us
    pallas_call x1, Pallas kernels, shards(): pl.pallas_call(place_kernel, grid_spec=pltpu.PrefetchScalarGridSpec(num_s...  10.6 us

profile of v1, /device:TPU:9, one launch (start us, length us, event | category | flops | bytes accessed | tf_op | source)
XLA Modules:
  0.0 280.9 jit_solution(1990311765709051420)
XLA Ops:
  0.0 0.8 select_reduce_fusion.3
  0.9 0.7 add_bitcast_fusion
  1.6 58.0 %all-gather.1 = s32[32,2,8]{2,1,0:T(2,128)S(1)} all-gather(s32[1,2,8]{2,1,0:T(2,128)S(1)} %add_bitcast_fusion), channel_id=2, replica_groups=mesh['gx'=4,'gy'=4,'gz'=2] {'gx','gy','gz'}, dimensions={0}, use_global_device_ids=true | all-gather | bytes 2112 | tf_op jit(solution)/shard_map/all_gather | solution.py:153
  59.5 0.7 slice_reduce_fusion
  60.2 0.1 reshape_squeeze.4
  60.2 0.1 copy.12
  60.3 0.1 copy.15
  60.4 0.1 reduce_sum.89
  60.5 0.1 reduce_sum.90
  60.6 0.2 convert_reduce_fusion.2
  60.8 0.7 convert_reduce_fusion.1
  61.5 0.1 copy.16
  61.5 0.1 convert_reduce_fusion
  61.6 0.2 fusion.7
  61.8 0.1 select_reduce_fusion.2
  62.0 0.1 copy.17
  62.1 0.1 reshape.188
  62.1 0.2 select_reduce_fusion.second_ref
  62.3 0.0 copy-start
  62.3 0.7 copy-done
  63.0 207.3 %exchange.1.block_ref = bf16[8,16,16,2048]{3,2,1,0:T(8,128)(2,1)} custom-call(s32[8]{0:T(128)S(1)} %get-tuple-element.10.first_ref, s32[8]{0:T(128)S(1)} %get-tuple-element.9.limit_ref, s32[16]{0:T(128)S(1)} %select_reduce_fusion.second_ref, bf16[8,128,2048]{2,1,0:T(8,128)(2,1)} %x_ref.1, f32[1,2048]{1,0:T(1,128)S(1)} %bitcast.13), custom_call_target="tpu_custom_call" | custom-call | tf_op jit(solution)/shard_map/exchange/pallas_call | solution.py:195
  270.3 10.6 %place.1 = bf16[16,128,2048]{2,1,0:T(8,128)(2,1)} custom-call(s32[16]{0:T(128)} %get-tuple-element.8.source_ref, s32[16]{0:T(128)} %get-tuple-element.7.filled_ref, bf16[8,16,16,2048]{3,2,1,0:T(8,128)(2,1)} %exchange.1.block_ref), custom_call_target="tpu_custom_call" | custom-call | tf_op jit(solution)/shard_map/place/pallas_call | solution.py:216
  (8 shorter events, 0.1 us)
Async XLA Ops:
  62.3 0.7 copy-start

commit v2 on v1

--- a/solution.py
+++ b/solution.py
@@ -124,18 +124,62 @@
         own_copy(c).wait()
 
 
-def place_kernel(source_ref, filled_ref, block_ref, out_ref):
-    chunks, _, rows, _ = block_ref.shape
-    slot = pl.program_id(0)
-
-    @pl.when(filled_ref[slot] == 1)
-    def _():
-        for c in range(chunks):
-            out_ref[0, pl.ds(c * rows, rows), :] = block_ref[c, 0]
-
-    @pl.when(filled_ref[slot] == 0)
-    def _():
-        out_ref[...] = jnp.zeros_like(out_ref)
+def gather_kernel(sizes, block_ref, all_ref, send_sem, recv_sem, own_sem):
+    nx, ny, depth = sizes
+    devices = nx * ny * depth
+    me = (lax.axis_index("gx") * ny + lax.axis_index("gy")) * depth + lax.axis_index("gz")
+
+    def copy(offset, peer, place):
+        return pltpu.make_async_remote_copy(
+            src_ref=block_ref,
+            dst_ref=all_ref.at[place],
+            send_sem=send_sem.at[offset],
+            recv_sem=recv_sem.at[offset],
+            device_id=(peer // (ny * depth), peer // depth % ny, peer % depth),
+            device_id_type=MESH,
+        )
+
+    @pl.loop(1, devices)
+    def _(offset):
+        copy(offset, lax.rem(me + offset, devices), me).start()
+
+    own = pltpu.make_async_copy(block_ref, all_ref.at[me], own_sem)
+    own.start()
+    own.wait()
+
+    @pl.loop(1, devices)
+    def _(offset):
+        origin = lax.rem(me + devices - offset, devices)
+        copy(offset, origin, origin).wait()
+
+
+def place_kernel(source_ref, filled_ref, blocks_ref, out_ref, held, zeros, in_sem, out_sem):
+    cap = out_ref.shape[0]
+
+    def fetch(slot):
+        return pltpu.make_async_copy(blocks_ref.at[:, source_ref[slot]], held.at[slot], in_sem.at[slot])
+
+    def store(slot):
+        return pltpu.make_async_copy(held.at[slot], out_ref.at[slot], out_sem.at[slot])
+
+    for slot in range(cap):
+        pl.when(filled_ref[slot] == 1)(lambda slot=slot: fetch(slot).start())
+    zeros[...] = jnp.zeros_like(zeros)
+    for slot in range(cap):
+
+        @pl.when(filled_ref[slot] == 0)
+        def _():
+            pltpu.make_async_copy(zeros, out_ref.at[slot], out_sem.at[slot]).start()
+
+    for slot in range(cap):
+
+        @pl.when(filled_ref[slot] == 1)
+        def _():
+            fetch(slot).wait()
+            store(slot).start()
+
+    for slot in range(cap):
+        store(slot).wait()
 
 
 def shards(embeds, dest_device, shuffle_key, lengths, gain):
@@ -150,11 +194,27 @@
     chunks = 8 if tile_rows % 128 == 0 else 1
     rows = tile_rows // chunks
 
-    both = lax.all_gather(
-        jnp.stack([dest_device, shuffle_key]), ("gx", "gy", "gz"), axis=0, tiled=False
-    )
-    dests = both[:, 0, :]
-    keys = both[:, 1, :]
+    smem = pl.BlockSpec(memory_space=pltpu.SMEM)
+    vmem = pl.BlockSpec(memory_space=pltpu.VMEM)
+    hbm = pl.BlockSpec(memory_space=pl.ANY)
+    devices = groups * depth
+    lanes = -(-2 * tiles_here // 128) * 128
+    block = jnp.pad(jnp.concatenate([dest_device, shuffle_key])[None, :], ((0, 0), (0, lanes - 2 * tiles_here)))
+    both = pl.pallas_call(
+        functools.partial(gather_kernel, (nx, ny, depth)),
+        out_shape=jax.ShapeDtypeStruct((devices, 1, lanes), jnp.int32),
+        in_specs=[vmem],
+        out_specs=vmem,
+        scratch_shapes=[
+            pltpu.SemaphoreType.DMA((devices,)),
+            pltpu.SemaphoreType.DMA((devices,)),
+            pltpu.SemaphoreType.DMA,
+        ],
+        compiler_params=pltpu.CompilerParams(has_side_effects=True),
+        name="gather_tables",
+    )(block)
+    dests = both[:, 0, :tiles_here]
+    keys = both[:, 0, tiles_here : 2 * tiles_here]
     depths = dests % depth
     order = jnp.arange(tiles_here, dtype=jnp.int32)
     before = (depths[:, None, :] == depths[:, :, None]) & (order[None, None, :] < order[None, :, None])
@@ -189,14 +249,11 @@
     source = jnp.sum(jnp.where(at, jnp.arange(groups, dtype=jnp.int32)[None, :], 0), axis=1).astype(jnp.int32)
     filled = jnp.sum(at.astype(jnp.int32), axis=1).astype(jnp.int32)
 
-    smem = pl.BlockSpec(memory_space=pltpu.SMEM)
-    vmem = pl.BlockSpec(memory_space=pltpu.VMEM)
-    sent = chunks * groups * rows * width * 2
     received = pl.pallas_call(
         functools.partial(exchange_kernel, (nx, ny, depth, per_peer, chunks, rows)),
         out_shape=jax.ShapeDtypeStruct((chunks, groups, rows, width), jnp.bfloat16),
         in_specs=[smem, smem, smem, vmem, vmem],
-        out_specs=pl.BlockSpec(memory_space=pl.ANY),
+        out_specs=hbm,
         scratch_shapes=[
             pltpu.VMEM((chunks, depth - 1, per_peer, rows, width), jnp.bfloat16),
             pltpu.VMEM((chunks, groups, rows, width), jnp.bfloat16),
@@ -213,19 +270,21 @@
         name="exchange",
     )(first, limits, second, embeds, gain.reshape(1, width))
 
-    return pl.pallas_call(
+    packed = pl.pallas_call(
         place_kernel,
-        grid_spec=pltpu.PrefetchScalarGridSpec(
-            num_scalar_prefetch=2,
-            grid=(cap,),
-            in_specs=[
-                pl.BlockSpec((chunks, 1, rows, width), lambda s, source, filled: (0, source[s], 0, 0))
-            ],
-            out_specs=pl.BlockSpec((1, tile_rows, width), lambda s, source, filled: (s, 0, 0)),
-        ),
-        out_shape=jax.ShapeDtypeStruct((cap, tile_rows, width), jnp.bfloat16),
+        out_shape=jax.ShapeDtypeStruct((cap, chunks, rows, width), jnp.bfloat16),
+        in_specs=[smem, smem, hbm],
+        out_specs=hbm,
+        scratch_shapes=[
+            pltpu.VMEM((cap, chunks, rows, width), jnp.bfloat16),
+            pltpu.VMEM((chunks, rows, width), jnp.bfloat16),
+            pltpu.SemaphoreType.DMA((cap,)),
+            pltpu.SemaphoreType.DMA((cap,)),
+        ],
+        compiler_params=pltpu.CompilerParams(vmem_limit_bytes=52 * 1024 * 1024),
         name="place",
     )(source, filled, received)
+    return packed.reshape(cap, tile_rows, width)
 
 
 def solution(mesh):

time: 282 us -> 225 us (0.80)
  blocking collectives: 58 us -> 0 us
    all_gather x1 -> x0, blocking collectives: 58 us -> none  [shards(): lax.all_gather(jnp.stack([dest_device, shuffle_key]), ('gx', 'gy', 'gz'),...]
    pallas_call x1 -> x2, Pallas kernels: 10.6 us -> 20.5 us  [the longest x1 13.7 us: shards(): pl.pallas_call(functools.partial(gather_kernel, (nx, ny, depth)), out_sha...]
    pallas_call x1, Pallas kernels: 207 us -> 198 us  [shards(): pl.pallas_call(functools.partial(exchange_kernel, (nx, ny, depth, per_pee...]
where the time goes in v2:
time: 225 us
  Pallas kernels  219 us (97%)
  other arithmetic  4.23 us (2%)
    pallas_call x1, Pallas kernels, shards(): pl.pallas_call(functools.partial(exchange_kernel, (nx, ny, depth, per_pee...  198 us
    pallas_call x1, Pallas kernels, shards(): pl.pallas_call(functools.partial(gather_kernel, (nx, ny, depth)), out_sha...  13.7 us
    pallas_call x1, Pallas kernels, shards(): pl.pallas_call(place_kernel, out_shape=jax.ShapeDtypeStruct((cap, chunks,...  6.77 us

profile of v2, /device:TPU:9, one launch (start us, length us, event | category | flops | bytes accessed | tf_op | source)
XLA Modules:
  0.0 224.7 jit_solution(430665304308820117)
XLA Ops:
  0.0 0.7 add_bitcast_fusion
  0.8 0.5 pad.4.block_ref
  1.3 0.8 select_reduce_fusion.3
  2.1 13.7 %gather_tables.1 = s32[32,1,128]{2,1,0:T(1,128)} custom-call(s32[1,128]{1,0:T(1,128)} %pad.4.block_ref), custom_call_target="tpu_custom_call" | custom-call | tf_op jit(solution)/shard_map/gather_tables/pallas_call | solution.py:203
  15.9 1.5 slice_reduce_fusion
  17.4 0.1 reshape_squeeze.4
  17.5 0.1 copy.12
  17.6 0.1 copy.15
  17.6 0.1 reduce_sum.89
  17.7 0.1 reduce_sum.90
  17.9 0.2 convert_reduce_fusion.2
  18.0 0.1 convert_reduce_fusion.1
  18.2 0.1 copy.16
  18.3 0.1 convert_reduce_fusion
  18.4 0.2 fusion.7
  18.5 0.1 select_reduce_fusion.2
  18.7 0.1 copy.17
  18.8 0.1 reshape.191
  18.9 0.2 select_reduce_fusion.second_ref
  19.0 0.0 copy-start
  19.0 0.7 copy-done
  19.7 198.1 %exchange.1.blocks_ref = bf16[8,16,16,2048]{3,2,1,0:T(8,128)(2,1)} custom-call(s32[8]{0:T(128)S(1)} %get-tuple-element.10.first_ref, s32[8]{0:T(128)S(1)} %get-tuple-element.9.limit_ref, s32[16]{0:T(128)S(1)} %select_reduce_fusion.second_ref, bf16[8,128,2048]{2,1,0:T(8,128)(2,1)} %x_ref.1, f32[1,2048]{1,0:T(1,128)S(1)} %bitcast.12), custom_call_target="tpu_custom_call" | custom-call | tf_op jit(solution)/shard_map/exchange/pallas_call | solution.py:252
  217.9 6.8 %place.1 = bf16[16,8,16,2048]{3,2,1,0:T(8,128)(2,1)} custom-call(s32[16]{0:T(128)S(1)} %get-tuple-element.8.source_ref, s32[16]{0:T(128)S(1)} %get-tuple-element.7.filled_ref, bf16[8,16,16,2048]{3,2,1,0:T(8,128)(2,1)} %exchange.1.blocks_ref), custom_call_target="tpu_custom_call" | custom-call | tf_op jit(solution)/shard_map/place/pallas_call | solution.py:273
  (8 shorter events, 0.1 us)
Async XLA Ops:
  19.0 0.7 copy-start

commit v3 on v2

v3 whole, which is shorter than its diff:
```python
import functools

import jax
import jax.numpy as jnp
from jax import lax
from jax.experimental import pallas as pl
from jax.experimental.pallas import tpu as pltpu
from jax.sharding import PartitionSpec as P

TILES_SEQ = 32
MESH = pl.DeviceIdType.MESH


def exchange_kernel(
    sizes, first_ref, limit_ref, note_ref, x_ref, gain_ref, recv_ref, keys_ref,
    first, outgoing, notes, note_table, second, keys_out, y_send, y_recv, g_send, g_recv, own_sem,
    note_send, note_recv, note_sem, key_send, key_recv, *arrived,
):
    nx, ny, depth, per_peer, chunks, rows = sizes
    groups = nx * ny
    gx, gy, gz = lax.axis_index("gx"), lax.axis_index("gy"), lax.axis_index("gz")
    group = gx * ny + gy
    offsets = [(dx, dy) for dy in sorted(range(ny), key=lambda d: abs(d - ny // 2)) for dx in range(nx)]
    offsets.remove((0, 0))

    def normed(c, slot):
        tile = first_ref[slot]
        values = x_ref[tile, pl.ds(c * rows, rows), :].astype(jnp.float32)
        meansq = jnp.mean(values * values, axis=-1, keepdims=True)
        scaled = values * lax.rsqrt(jnp.maximum(meansq, 0.25)) * gain_ref[...]
        row = c * rows + lax.broadcasted_iota(jnp.int32, (rows, 1), 0)
        return jnp.where(row < limit_ref[slot], scaled, 0.0).astype(jnp.bfloat16)

    def y_copy(c, dz):
        peer = lax.rem(gz + dz, depth)
        return pltpu.make_async_remote_copy(
            src_ref=first.at[c, dz - 1],
            dst_ref=arrived[c].at[pl.ds(gz * per_peer, per_peer)],
            send_sem=y_send.at[c, dz - 1],
            recv_sem=y_recv.at[c, dz - 1],
            device_id=(gx, gy, peer),
            device_id_type=MESH,
        )

    def y_wait(c, dz):
        origin = lax.rem(gz + depth - dz, depth)
        pltpu.make_async_remote_copy(
            src_ref=first.at[c, dz - 1],
            dst_ref=arrived[c].at[pl.ds(origin * per_peer, per_peer)],
            send_sem=y_send.at[c, dz - 1],
            recv_sem=y_recv.at[c, dz - 1],
            device_id=(gx, gy, origin),
            device_id_type=MESH,
        ).wait_recv()

    def peer_of(k):
        dx, dy = offsets[k]
        return lax.rem(gx + dx, nx), lax.rem(gy + dy, ny)

    def g_copy(c, k):
        px, py = peer_of(k)
        return pltpu.make_async_remote_copy(
            src_ref=outgoing.at[c, k],
            dst_ref=recv_ref.at[c, group],
            send_sem=g_send.at[c, k],
            recv_sem=g_recv.at[c, k],
            device_id=(px, py, gz),
            device_id_type=MESH,
        )

    def own_copy(c):
        return pltpu.make_async_copy(outgoing.at[c, groups - 1], recv_ref.at[c, group], own_sem.at[c])

    def note_copy(dz, peer, place):
        return pltpu.make_async_remote_copy(
            src_ref=note_ref.at[peer],
            dst_ref=notes.at[place],
            send_sem=note_send.at[dz - 1],
            recv_sem=note_recv.at[dz - 1],
            device_id=(gx, gy, peer),
            device_id_type=MESH,
        )

    def key_copy(k, px, py, place):
        return pltpu.make_async_remote_copy(
            src_ref=keys_out.at[k],
            dst_ref=keys_ref.at[place],
            send_sem=key_send.at[k],
            recv_sem=key_recv.at[k],
            device_id=(px, py, gz),
            device_id_type=MESH,
        )

    def prepare(c):
        for dz in range(1, depth):
            peer = lax.rem(gz + dz, depth)
            for p in range(per_peer):
                first[c, dz - 1, p] = normed(c, peer * per_peer + p)
        for p in range(per_peer):
            arrived[c][gz * per_peer + p] = normed(c, gz * per_peer + p)

    def send_first(c):
        for dz in range(1, depth):
            y_copy(c, dz).start()

    def find_slots():
        for dz in range(1, depth):
            origin = lax.rem(gz + depth - dz, depth)
            note_copy(dz, origin, origin).wait()
        tables = [
            pltpu.make_async_copy(
                notes.at[lax.rem(gz + dz, depth)], note_table.at[lax.rem(gz + dz, depth)], note_sem.at[dz]
            )
            for dz in range(1, depth)
        ]
        tables.append(pltpu.make_async_copy(note_ref.at[gz], note_table.at[gz], note_sem.at[0]))
        for copy in tables:
            copy.start()
        for copy in tables:
            copy.wait()

        for k in range(groups):
            px, py = peer_of(k) if k < groups - 1 else (gx, gy)
            wanted = px * ny + py
            slot, key = jnp.int32(0), jnp.int32(0)
            for z in range(depth):
                for p in range(per_peer):
                    hit = note_table[z, 0, p] == wanted
                    slot = jnp.where(hit, z * per_peer + p, slot)
                    key = jnp.where(hit, note_table[z, 0, per_peer + p], key)
            second[k] = slot
            row = jnp.full(keys_out.shape[1:], key, jnp.int32)
            if k < groups - 1:
                keys_out[k] = row
            else:
                keys_ref[group] = row

    def forward(c):
        for dz in range(1, depth):
            y_wait(c, dz)
        for k in range(groups):
            outgoing[c, k] = arrived[c][second[k]]
        for k in range(groups - 1):
            g_copy(c, k).start()
        own_copy(c).start()

    barrier = pltpu.get_barrier_semaphore()
    for dz in range(1, depth):
        pl.semaphore_signal(
            barrier, inc=1, device_id=(gx, gy, lax.rem(gz + dz, depth)), device_id_type=MESH
        )
    for k in range(groups - 1):
        px, py = peer_of(k)
        pl.semaphore_signal(barrier, inc=1, device_id=(px, py, gz), device_id_type=MESH)
    prepare(0)
    pl.semaphore_wait(barrier, depth - 1 + groups - 1)
    for dz in range(1, depth):
        note_copy(dz, lax.rem(gz + dz, depth), gz).start()
    send_first(0)
    if chunks > 1:
        prepare(1)
        send_first(1)
    find_slots()
    forward(0)
    for k in range(groups - 1):
        px, py = peer_of(k)
        key_copy(k, px, py, group).start()
    for c in range(2, chunks):
        prepare(c)
        send_first(c)
        forward(c - 1)
    if chunks > 1:
        forward(chunks - 1)

    for c in range(chunks):
        for dz in range(1, depth):
            y_copy(c, dz).wait_send()
    sources = []
    for dx, dy in offsets:
        sources.append((lax.rem(gx + nx - dx, nx), lax.rem(gy + ny - dy, ny)))
    for k, (sx, sy) in enumerate(sources):
        key_copy(k, sx, sy, sx * ny + sy).wait()

    @pl.loop(0, chunks)
    def _(c):
        for k, (sx, sy) in enumerate(sources):
            g_copy(c, k).wait_send()
            pltpu.make_async_remote_copy(
                src_ref=outgoing.at[c, k],
                dst_ref=recv_ref.at[c, sx * ny + sy],
                send_sem=g_send.at[c, k],
                recv_sem=g_recv.at[c, k],
                device_id=(sx, sy, gz),
                device_id_type=MESH,
            ).wait_recv()
        own_copy(c).wait()


def place_kernel(source_ref, filled_ref, blocks_ref, out_ref, held, zeros, in_sem, out_sem):
    cap = out_ref.shape[0]

    def fetch(slot):
        return pltpu.make_async_copy(blocks_ref.at[:, source_ref[slot]], held.at[slot], in_sem.at[slot])

    def store(slot):
        return pltpu.make_async_copy(held.at[slot], out_ref.at[slot], out_sem.at[slot])

    for slot in range(cap):
        pl.when(filled_ref[slot] == 1)(lambda slot=slot: fetch(slot).start())
    zeros[...] = jnp.zeros_like(zeros)
    for slot in range(cap):

        @pl.when(filled_ref[slot] == 0)
        def _():
            pltpu.make_async_copy(zeros, out_ref.at[slot], out_sem.at[slot]).start()

    for slot in range(cap):

        @pl.when(filled_ref[slot] == 1)
        def _():
            fetch(slot).wait()
            store(slot).start()

    for slot in range(cap):
        store(slot).wait()


def shards(embeds, dest_device, shuffle_key, lengths, gain):
    tiles_here, tile_rows, width = embeds.shape
    nx, ny, depth = lax.axis_size("gx"), lax.axis_size("gy"), lax.axis_size("gz")
    groups = nx * ny
    group = lax.axis_index("gx") * ny + lax.axis_index("gy")
    gz = lax.axis_index("gz")
    me = group * depth + gz
    per_peer = (tiles_here + depth - 1) // depth
    slots = depth * per_peer
    chunks = 8 if tile_rows % 128 == 0 else 1
    rows = tile_rows // chunks

    smem = pl.BlockSpec(memory_space=pltpu.SMEM)
    vmem = pl.BlockSpec(memory_space=pltpu.VMEM)
    hbm = pl.BlockSpec(memory_space=pl.ANY)
    order = jnp.arange(tiles_here, dtype=jnp.int32)
    depths = dest_device % depth
    before = (depths[None, :] == depths[:, None]) & (order[None, :] < order[:, None])
    spot = jnp.sum(before.astype(jnp.int32), axis=1)
    here_slot = depths * per_peer + spot
    hit = here_slot[None, :] == jnp.arange(slots, dtype=jnp.int32)[:, None]
    tile_ids = me * tiles_here + order
    match = (tile_ids // TILES_SEQ)[:, None] == jnp.arange(lengths.shape[0], dtype=jnp.int32)[None, :]
    limit = jnp.sum(jnp.where(match, lengths[None, :], 0), axis=1) - tile_ids % TILES_SEQ * tile_rows
    first = jnp.sum(jnp.where(hit, order[None, :], 0), axis=1).astype(jnp.int32)
    limits = jnp.sum(jnp.where(hit, jnp.maximum(limit, 0)[None, :], 0), axis=1).astype(jnp.int32)
    slot_group = jnp.sum(jnp.where(hit, dest_device[None, :] // depth + 1, 0), axis=1) - 1
    slot_key = jnp.sum(jnp.where(hit, shuffle_key[None, :] + 1, 0), axis=1)
    lanes = -(-2 * per_peer // 128) * 128
    note = jnp.concatenate([slot_group.reshape(depth, per_peer), slot_key.reshape(depth, per_peer)], axis=1)
    note = jnp.pad(note.astype(jnp.int32), ((0, 0), (0, lanes - 2 * per_peer)))[:, None, :]

    received, key_rows = pl.pallas_call(
        functools.partial(exchange_kernel, (nx, ny, depth, per_peer, chunks, rows)),
        out_shape=(
            jax.ShapeDtypeStruct((chunks, groups, rows, width), jnp.bfloat16),
            jax.ShapeDtypeStruct((groups, 1, 128), jnp.int32),
        ),
        in_specs=[smem, smem, vmem, vmem, vmem],
        out_specs=(hbm, vmem),
        scratch_shapes=[
            pltpu.VMEM((chunks, depth - 1, per_peer, rows, width), jnp.bfloat16),
            pltpu.VMEM((chunks, groups, rows, width), jnp.bfloat16),
            pltpu.VMEM((depth, 1, lanes), jnp.int32),
            pltpu.SMEM((depth, 1, lanes), jnp.int32),
            pltpu.SMEM((groups,), jnp.int32),
            pltpu.VMEM((groups, 1, 128), jnp.int32),
            pltpu.SemaphoreType.DMA((chunks, depth - 1)),
            pltpu.SemaphoreType.DMA((chunks, depth - 1)),
            pltpu.SemaphoreType.DMA((chunks, groups)),
            pltpu.SemaphoreType.DMA((chunks, groups)),
            pltpu.SemaphoreType.DMA((chunks,)),
            pltpu.SemaphoreType.DMA((depth,)),
            pltpu.SemaphoreType.DMA((depth,)),
            pltpu.SemaphoreType.DMA((depth,)),
            pltpu.SemaphoreType.DMA((groups,)),
            pltpu.SemaphoreType.DMA((groups,)),
        ]
        + [pltpu.VMEM((slots, rows, width), jnp.bfloat16)] * chunks,
        compiler_params=pltpu.CompilerParams(
            collective_id=0, has_side_effects=True, vmem_limit_bytes=52 * 1024 * 1024
        ),
        name="exchange",
    )(first, limits, note, embeds, gain.reshape(1, width))

    key_of = key_rows[:, 0, 0]
    valid = key_of > 0
    rank = jnp.sum((valid[None, :] & (key_of[None, :] < key_of[:, None])).astype(jnp.int32), axis=1)
    cap = 2 * tiles_here
    at = valid[None, :] & (rank[None, :] == jnp.arange(cap, dtype=jnp.int32)[:, None])
    source = jnp.sum(jnp.where(at, jnp.arange(groups, dtype=jnp.int32)[None, :], 0), axis=1).astype(jnp.int32)
    filled = jnp.sum(at.astype(jnp.int32), axis=1).astype(jnp.int32)

    packed = pl.pallas_call(
        place_kernel,
        out_shape=jax.ShapeDtypeStruct((cap, chunks, rows, width), jnp.bfloat16),
        in_specs=[smem, smem, hbm],
        out_specs=hbm,
        scratch_shapes=[
            pltpu.VMEM((cap, chunks, rows, width), jnp.bfloat16),
            pltpu.VMEM((chunks, rows, width), jnp.bfloat16),
            pltpu.SemaphoreType.DMA((cap,)),
            pltpu.SemaphoreType.DMA((cap,)),
        ],
        compiler_params=pltpu.CompilerParams(vmem_limit_bytes=52 * 1024 * 1024),
        name="place",
    )(source, filled, received)
    return packed.reshape(cap, tile_rows, width)


def solution(mesh):
    return jax.shard_map(
        shards,
        mesh=mesh,
        in_specs=(
            P(("gx", "gy", "gz"), None, None),
            P(("gx", "gy", "gz")),
            P(("gx", "gy", "gz")),
            P(),
            P(),
        ),
        out_specs=P(("gx", "gy", "gz"), None, None),
        check_vma=False,
    )
```

time: 225 us -> 209 us (0.929)
  Pallas kernels: 219 us -> 204 us
    pallas_call x1 -> x0, Pallas kernels: 13.7 us -> none  [shards(): pl.pallas_call(functools.partial(gather_kernel, (nx, ny, depth)), out_sha...]
where the time goes in v3:
time: 209 us; the launch traced here: 208 us
  Pallas kernels  204 us (98%)
  other arithmetic  2.91 us (1%)
    pallas_call x1, Pallas kernels, shards(): pl.pallas_call(functools.partial(exchange_kernel, (nx, ny, depth, per_pee...  198 us
    pallas_call x1, Pallas kernels, shards(): pl.pallas_call(place_kernel, out_shape=jax.ShapeDtypeStruct((cap, chunks,...  6.01 us

profile of v3, /device:TPU:9, one launch (start us, length us, event | category | flops | bytes accessed | tf_op | source)
XLA Modules:
  0.0 208.2 jit_solution(11506265029075183868)
XLA Ops:
  0.0 0.7 broadcast_add_fusion.1
  0.7 0.8 select_reduce_fusion.4
  1.5 0.7 and_select_fusion.3
  2.2 0.2 convert_reduce_fusion.2
  2.4 0.1 select_reduce_fusion.2
  2.5 0.1 sub.24
  2.6 0.1 reshape.86
  2.7 0.1 pad_add_fusion
  2.8 0.0 copy-start
  2.8 0.7 copy-done
  3.5 198.0 %exchange.1 = (bf16[8,16,16,2048]{3,2,1,0:T(8,128)(2,1)}, s32[16,1,128]{2,1,0:T(1,128)S(1)}) custom-call(s32[8]{0:T(128)S(1)} %get-tuple-element.14.first_ref, s32[8]{0:T(128)S(1)} %get-tuple-element.13.limit_ref, s32[2,1,128]{2,1,0:T(1,128)S(1)} %bitcast.4, bf16[8,128,2048]{2,1,0:T(8,128)(2,1)} %x_ref.1, f32[1,2048]{1,0:T(1,128)S(1)} %bitcast.3), custom_call_target="tpu_custom_call" | custom-call | tf_op jit(solution)/shard_map/exchange/pallas_call | solution.py:260
  201.5 0.4 slice_reduce_fusion
  201.9 0.2 convert_reduce_fusion.1
  202.1 0.1 convert_reduce_fusion
  202.2 6.0 %place.1 = bf16[16,8,16,2048]{3,2,1,0:T(8,128)(2,1)} custom-call(s32[16]{0:T(128)S(1)} %get-tuple-element.10.source_ref, s32[16]{0:T(128)S(1)} %get-tuple-element.9.filled_ref, bf16[8,16,16,2048]{3,2,1,0:T(8,128)(2,1)} %get-tuple-element.8.blocks_ref), custom_call_target="tpu_custom_call" | custom-call | tf_op jit(solution)/shard_map/place/pallas_call | solution.py:301
  (5 shorter events, 0.0 us)
Async XLA Ops:
  2.8 0.7 copy-start

commit v4 on v3

v4 whole, which is shorter than its diff:
```python
import functools

import jax
import jax.numpy as jnp
from jax import lax
from jax.experimental import pallas as pl
from jax.experimental.pallas import tpu as pltpu
from jax.sharding import PartitionSpec as P

TILES_SEQ = 32
MESH = pl.DeviceIdType.MESH


def exchange_kernel(
    sizes, dest_ref, order_ref, length_ref, x_ref, gain_ref, recv_ref, keys_ref,
    gain, first_table, limit_table, note_out, notes, note_table, second, keys_out,
    x_sem, gain_sem, y_send, y_recv, g_send, g_recv, own_sem,
    note_send, note_recv, note_sem, key_send, key_recv, *buffers,
):
    nx, ny, depth, per_peer, chunk_rows = sizes
    chunks = len(chunk_rows)
    starts = [sum(chunk_rows[:c]) for c in range(chunks)]
    groups = nx * ny
    tiles_here, tile_rows, _ = x_ref.shape
    raw, first, arrived, outgoing = (buffers[i * chunks : (i + 1) * chunks] for i in range(4))
    gx, gy, gz = lax.axis_index("gx"), lax.axis_index("gy"), lax.axis_index("gz")
    group = gx * ny + gy
    me = group * depth + gz
    offsets = [(dx, dy) for dy in sorted(range(ny), key=lambda d: abs(d - ny // 2)) for dx in range(nx)]
    offsets.remove((0, 0))

    def load(c):
        return pltpu.make_async_copy(
            x_ref.at[:, pl.ds(starts[c], chunk_rows[c])], raw[c], x_sem.at[c]
        )

    def fill_tables():
        depths = [lax.rem(dest_ref[i], depth) for i in range(tiles_here)]
        dest_groups = [lax.div(dest_ref[i], depth) for i in range(tiles_here)]
        places, limits = [], []
        for i in range(tiles_here):
            spot = jnp.int32(0)
            for j in range(i):
                spot = spot + jnp.where(depths[j] == depths[i], 1, 0)
            places.append(depths[i] * per_peer + spot)
            tile = me * tiles_here + i
            length = length_ref[tile // TILES_SEQ]
            limits.append(jnp.maximum(length - tile % TILES_SEQ * tile_rows, 0))
        lane = lax.broadcasted_iota(jnp.int32, note_out.shape[1:], 1)
        for z in range(depth):
            row = jnp.zeros(note_out.shape[1:], jnp.int32)
            for p in range(per_peer):
                slot = z * per_peer + p
                tile, limit, dest_group, key = (jnp.int32(v) for v in (0, 0, -1, 0))
                for i in range(tiles_here):
                    hit = places[i] == slot
                    tile = jnp.where(hit, i, tile)
                    limit = jnp.where(hit, limits[i], limit)
                    dest_group = jnp.where(hit, dest_groups[i], dest_group)
                    key = jnp.where(hit, order_ref[i] + 1, key)
                first_table[slot] = tile
                limit_table[slot] = limit
                row = jnp.where(lane == p, dest_group, row)
                row = jnp.where(lane == per_peer + p, key, row)
            note_out[z] = row

    def normed(c, slot):
        rows = chunk_rows[c]
        values = raw[c][first_table[slot]].astype(jnp.float32)
        meansq = jnp.mean(values * values, axis=-1, keepdims=True)
        scaled = values * lax.rsqrt(jnp.maximum(meansq, 0.25)) * gain[...]
        row = starts[c] + lax.broadcasted_iota(jnp.int32, (rows, 1), 0)
        return jnp.where(row < limit_table[slot], scaled, 0.0).astype(jnp.bfloat16)

    def y_copy(c, dz, peer, origin):
        return pltpu.make_async_remote_copy(
            src_ref=first[c].at[dz - 1],
            dst_ref=arrived[c].at[pl.ds(origin * per_peer, per_peer)],
            send_sem=y_send.at[c, dz - 1],
            recv_sem=y_recv.at[c, dz - 1],
            device_id=(gx, gy, peer),
            device_id_type=MESH,
        )

    def peer_of(k):
        dx, dy = offsets[k]
        return lax.rem(gx + dx, nx), lax.rem(gy + dy, ny)

    def g_copy(c, k, px, py, origin):
        return pltpu.make_async_remote_copy(
            src_ref=outgoing[c].at[k],
            dst_ref=recv_ref.at[origin, pl.ds(starts[c], chunk_rows[c])],
            send_sem=g_send.at[c, k],
            recv_sem=g_recv.at[c, k],
            device_id=(px, py, gz),
            device_id_type=MESH,
        )

    def own_copy(c):
        return pltpu.make_async_copy(
            outgoing[c].at[groups - 1],
            recv_ref.at[group, pl.ds(starts[c], chunk_rows[c])],
            own_sem.at[c],
        )

    def note_copy(dz, peer, place):
        return pltpu.make_async_remote_copy(
            src_ref=note_out.at[peer],
            dst_ref=notes.at[place],
            send_sem=note_send.at[dz - 1],
            recv_sem=note_recv.at[dz - 1],
            device_id=(gx, gy, peer),
            device_id_type=MESH,
        )

    def key_copy(k, px, py, place):
        return pltpu.make_async_remote_copy(
            src_ref=keys_out.at[k],
            dst_ref=keys_ref.at[place],
            send_sem=key_send.at[k],
            recv_sem=key_recv.at[k],
            device_id=(px, py, gz),
            device_id_type=MESH,
        )

    def prepare(c):
        load(c).wait()
        for dz in range(1, depth):
            peer = lax.rem(gz + dz, depth)
            for p in range(per_peer):
                first[c][dz - 1, p] = normed(c, peer * per_peer + p)
        for p in range(per_peer):
            arrived[c][gz * per_peer + p] = normed(c, gz * per_peer + p)

    def send_first(c):
        for dz in range(1, depth):
            y_copy(c, dz, lax.rem(gz + dz, depth), gz).start()

    def find_slots():
        for dz in range(1, depth):
            origin = lax.rem(gz + depth - dz, depth)
            note_copy(dz, origin, origin).wait()
        tables = [
            pltpu.make_async_copy(
                notes.at[lax.rem(gz + dz, depth)], note_table.at[lax.rem(gz + dz, depth)], note_sem.at[dz]
            )
            for dz in range(1, depth)
        ]
        tables.append(pltpu.make_async_copy(note_out.at[gz], note_table.at[gz], note_sem.at[0]))
        for copy in tables:
            copy.start()
        for copy in tables:
            copy.wait()

        for k in range(groups):
            px, py = peer_of(k) if k < groups - 1 else (gx, gy)
            wanted = px * ny + py
            slot, key = jnp.int32(0), jnp.int32(0)
            for z in range(depth):
                for p in range(per_peer):
                    hit = note_table[z, 0, p] == wanted
                    slot = jnp.where(hit, z * per_peer + p, slot)
                    key = jnp.where(hit, note_table[z, 0, per_peer + p], key)
            second[k] = slot
            row = jnp.full(keys_out.shape[1:], key, jnp.int32)
            if k < groups - 1:
                keys_out[k] = row
            else:
                keys_ref[group] = row

    def forward(c):
        for dz in range(1, depth):
            origin = lax.rem(gz + depth - dz, depth)
            y_copy(c, dz, origin, origin).wait_recv()
        for k in range(groups):
            outgoing[c][k] = arrived[c][second[k]]
        for k in range(groups - 1):
            px, py = peer_of(k)
            g_copy(c, k, px, py, group).start()
        own_copy(c).start()

    gain_copy = pltpu.make_async_copy(gain_ref, gain, gain_sem)
    gain_copy.start()
    for c in range(chunks):
        load(c).start()
    barrier = pltpu.get_barrier_semaphore()
    for dz in range(1, depth):
        pl.semaphore_signal(
            barrier, inc=1, device_id=(gx, gy, lax.rem(gz + dz, depth)), device_id_type=MESH
        )
    for k in range(groups - 1):
        px, py = peer_of(k)
        pl.semaphore_signal(barrier, inc=1, device_id=(px, py, gz), device_id_type=MESH)
    fill_tables()
    gain_copy.wait()
    prepare(0)
    pl.semaphore_wait(barrier, depth - 1 + groups - 1)
    for dz in range(1, depth):
        note_copy(dz, lax.rem(gz + dz, depth), gz).start()
    send_first(0)
    if chunks > 1:
        prepare(1)
        send_first(1)
    find_slots()
    forward(0)
    for k in range(groups - 1):
        px, py = peer_of(k)
        key_copy(k, px, py, group).start()
    for c in range(2, chunks):
        prepare(c)
        send_first(c)
        forward(c - 1)
    if chunks > 1:
        forward(chunks - 1)

    for c in range(chunks):
        for dz in range(1, depth):
            y_copy(c, dz, lax.rem(gz + dz, depth), gz).wait_send()
    sources = []
    for dx, dy in offsets:
        sources.append((lax.rem(gx + nx - dx, nx), lax.rem(gy + ny - dy, ny)))
    for k, (sx, sy) in enumerate(sources):
        key_copy(k, sx, sy, sx * ny + sy).wait()
    for c in range(chunks):
        for k, (sx, sy) in enumerate(sources):
            g_copy(c, k, sx, sy, sx * ny + sy).wait()
        own_copy(c).wait()


def place_kernel(source_ref, filled_ref, blocks_ref, out_ref, held, zeros, in_sem, out_sem):
    cap = out_ref.shape[0]

    def fetch(slot):
        return pltpu.make_async_copy(blocks_ref.at[source_ref[slot]], held.at[slot], in_sem.at[slot])

    def store(slot):
        return pltpu.make_async_copy(held.at[slot], out_ref.at[slot], out_sem.at[slot])

    for slot in range(cap):
        pl.when(filled_ref[slot] == 1)(lambda slot=slot: fetch(slot).start())
    zeros[...] = jnp.zeros_like(zeros)
    for slot in range(cap):

        @pl.when(filled_ref[slot] == 0)
        def _():
            pltpu.make_async_copy(zeros, out_ref.at[slot], out_sem.at[slot]).start()

    for slot in range(cap):

        @pl.when(filled_ref[slot] == 1)
        def _():
            fetch(slot).wait()
            store(slot).start()

    for slot in range(cap):
        store(slot).wait()


def shards(embeds, dest_device, shuffle_key, lengths, gain):
    tiles_here, tile_rows, width = embeds.shape
    nx, ny, depth = lax.axis_size("gx"), lax.axis_size("gy"), lax.axis_size("gz")
    groups = nx * ny
    per_peer = (tiles_here + depth - 1) // depth
    slots = depth * per_peer
    chunk_rows = (tile_rows,)
    if tile_rows % 128 == 0:
        chunk_rows = tuple(part * tile_rows // 16 for part in (1, 1, 2, 2, 4, 4, 2))
    chunks = len(chunk_rows)

    smem = pl.BlockSpec(memory_space=pltpu.SMEM)
    vmem = pl.BlockSpec(memory_space=pltpu.VMEM)
    hbm = pl.BlockSpec(memory_space=pl.ANY)
    lanes = -(-2 * per_peer // 128) * 128
    received, key_rows = pl.pallas_call(
        functools.partial(exchange_kernel, (nx, ny, depth, per_peer, chunk_rows)),
        out_shape=(
            jax.ShapeDtypeStruct((groups, tile_rows, width), jnp.bfloat16),
            jax.ShapeDtypeStruct((groups, 1, 128), jnp.int32),
        ),
        in_specs=[smem, smem, smem, hbm, hbm],
        out_specs=(hbm, vmem),
        scratch_shapes=[
            pltpu.VMEM((1, width), jnp.float32),
            pltpu.SMEM((slots,), jnp.int32),
            pltpu.SMEM((slots,), jnp.int32),
            pltpu.VMEM((depth, 1, lanes), jnp.int32),
            pltpu.VMEM((depth, 1, lanes), jnp.int32),
            pltpu.SMEM((depth, 1, lanes), jnp.int32),
            pltpu.SMEM((groups,), jnp.int32),
            pltpu.VMEM((groups, 1, 128), jnp.int32),
            pltpu.SemaphoreType.DMA((chunks,)),
            pltpu.SemaphoreType.DMA,
            pltpu.SemaphoreType.DMA((chunks, depth - 1)),
            pltpu.SemaphoreType.DMA((chunks, depth - 1)),
            pltpu.SemaphoreType.DMA((chunks, groups)),
            pltpu.SemaphoreType.DMA((chunks, groups)),
            pltpu.SemaphoreType.DMA((chunks,)),
            pltpu.SemaphoreType.DMA((depth,)),
            pltpu.SemaphoreType.DMA((depth,)),
            pltpu.SemaphoreType.DMA((depth,)),
            pltpu.SemaphoreType.DMA((groups,)),
            pltpu.SemaphoreType.DMA((groups,)),
        ]
        + [pltpu.VMEM((tiles_here, rows, width), jnp.bfloat16) for rows in chunk_rows]
        + [pltpu.VMEM((depth - 1, per_peer, rows, width), jnp.bfloat16) for rows in chunk_rows]
        + [pltpu.VMEM((slots, rows, width), jnp.bfloat16) for rows in chunk_rows]
        + [pltpu.VMEM((groups, rows, width), jnp.bfloat16) for rows in chunk_rows],
        compiler_params=pltpu.CompilerParams(
            collective_id=0, has_side_effects=True, vmem_limit_bytes=52 * 1024 * 1024
        ),
        name="exchange",
    )(dest_device, shuffle_key, lengths, embeds, gain.reshape(1, width))

    key_of = key_rows[:, 0, 0]
    valid = key_of > 0
    rank = jnp.sum((valid[None, :] & (key_of[None, :] < key_of[:, None])).astype(jnp.int32), axis=1)
    cap = 2 * tiles_here
    at = valid[None, :] & (rank[None, :] == jnp.arange(cap, dtype=jnp.int32)[:, None])
    source = jnp.sum(jnp.where(at, jnp.arange(groups, dtype=jnp.int32)[None, :], 0), axis=1).astype(jnp.int32)
    filled = jnp.sum(at.astype(jnp.int32), axis=1).astype(jnp.int32)

    return pl.pallas_call(
        place_kernel,
        out_shape=jax.ShapeDtypeStruct((cap, tile_rows, width), jnp.bfloat16),
        in_specs=[smem, smem, hbm],
        out_specs=hbm,
        scratch_shapes=[
            pltpu.VMEM((cap, tile_rows, width), jnp.bfloat16),
            pltpu.VMEM((tile_rows, width), jnp.bfloat16),
            pltpu.SemaphoreType.DMA((cap,)),
            pltpu.SemaphoreType.DMA((cap,)),
        ],
        compiler_params=pltpu.CompilerParams(vmem_limit_bytes=52 * 1024 * 1024),
        name="place",
    )(source, filled, received)


def solution(mesh):
    return jax.shard_map(
        shards,
        mesh=mesh,
        in_specs=(
            P(("gx", "gy", "gz"), None, None),
            P(("gx", "gy", "gz")),
            P(("gx", "gy", "gz")),
            P(),
            P(),
        ),
        out_specs=P(("gx", "gy", "gz"), None, None),
        check_vma=False,
    )
```

time: 209 us -> 204 us (0.976)
  Pallas kernels: 204 us -> 200 us
  other arithmetic: 2.91 us -> 0.32 us
    pallas_call x1, Pallas kernels: 198 us -> 193 us  [shards(): pl.pallas_call(functools.partial(exchange_kernel, (nx, ny, depth, per_pee...]
where the time goes in v4:
time: 204 us; the launch traced here: 203 us
  Pallas kernels  200 us (98%)
  local copies, waits for them, and re-layouts  3.04 us (1%)
    pallas_call x1, Pallas kernels, shards(): pl.pallas_call(functools.partial(exchange_kernel, (nx, ny, depth, per_pee...  193 us
    pallas_call x1, Pallas kernels, shards(): pl.pallas_call(place_kernel, out_shape=jax.ShapeDtypeStruct((cap, tile_ro...  6.64 us

profile of v4, /device:TPU:9, one launch (start us, length us, event | category | flops | bytes accessed | tf_op | source)
XLA Modules:
  0.0 203.4 jit_solution(3513753911612072482)
XLA Ops:
  0.0 0.0 copy-start
  0.0 0.7 copy-done
  0.7 0.0 copy-start.1
  0.7 0.7 copy-done.1
  1.4 0.0 copy-start.2
  1.4 0.7 copy-done.2
  2.0 0.0 copy-start.3
  2.0 0.7 copy-done.3
  2.7 193.4 %exchange.1 = (bf16[16,128,2048]{2,1,0:T(8,128)(2,1)}, s32[16,1,128]{2,1,0:T(1,128)S(1)}) custom-call(s32[8]{0:T(128)S(1)} %copy-done.1, s32[8]{0:T(128)S(1)} %copy-done.2, s32[8]{0:T(128)S(1)} %copy-done.3, bf16[8,128,2048]{2,1,0:T(8,128)(2,1)} %x_ref.1, f32[1,2048]{1,0:T(1,128)S(1)} %bitcast.1), custom_call_target="tpu_custom_call" | custom-call | tf_op jit(solution)/shard_map/exchange/pallas_call | solution.py:274
  196.0 0.4 slice_reduce_fusion
  196.4 0.2 convert_reduce_fusion.1
  196.6 0.1 convert_reduce_fusion
  196.7 6.6 %place.1 = bf16[16,128,2048]{2,1,0:T(8,128)(2,1)} custom-call(s32[16]{0:T(128)S(1)} %get-tuple-element.10.source_ref, s32[16]{0:T(128)S(1)} %get-tuple-element.9.filled_ref, bf16[16,128,2048]{2,1,0:T(8,128)(2,1)} %get-tuple-element.8.blocks_ref), custom_call_target="tpu_custom_call" | custom-call | tf_op jit(solution)/shard_map/place/pallas_call | solution.py:322
  (1 shorter events, 0.0 us)
Async XLA Ops:
  0.0 0.7 copy-start
  0.7 0.7 copy-start.1
  1.4 0.7 copy-start.2
  2.0 0.7 copy-start.3

commit v5 on v4

--- a/solution.py
+++ b/solution.py
@@ -12,8 +12,8 @@
 
 
 def exchange_kernel(
-    sizes, dest_ref, order_ref, length_ref, x_ref, gain_ref, recv_ref, keys_ref,
-    gain, first_table, limit_table, note_out, notes, note_table, second, keys_out,
+    sizes, small_in, x_ref, gain_ref, recv_ref, keys_ref,
+    small_ref, gain, small_sem, first_table, limit_table, note_out, notes, note_table, second, keys_out,
     x_sem, gain_sem, y_send, y_recv, g_send, g_recv, own_sem,
     note_send, note_recv, note_sem, key_send, key_recv, *buffers,
 ):
@@ -35,8 +35,8 @@
         )
 
     def fill_tables():
-        depths = [lax.rem(dest_ref[i], depth) for i in range(tiles_here)]
-        dest_groups = [lax.div(dest_ref[i], depth) for i in range(tiles_here)]
+        depths = [lax.rem(small_ref[0, i], depth) for i in range(tiles_here)]
+        dest_groups = [lax.div(small_ref[0, i], depth) for i in range(tiles_here)]
         places, limits = [], []
         for i in range(tiles_here):
             spot = jnp.int32(0)
@@ -44,7 +44,7 @@
                 spot = spot + jnp.where(depths[j] == depths[i], 1, 0)
             places.append(depths[i] * per_peer + spot)
             tile = me * tiles_here + i
-            length = length_ref[tile // TILES_SEQ]
+            length = small_ref[0, 2 * tiles_here + tile // TILES_SEQ]
             limits.append(jnp.maximum(length - tile % TILES_SEQ * tile_rows, 0))
         lane = lax.broadcasted_iota(jnp.int32, note_out.shape[1:], 1)
         for z in range(depth):
@@ -57,7 +57,7 @@
                     tile = jnp.where(hit, i, tile)
                     limit = jnp.where(hit, limits[i], limit)
                     dest_group = jnp.where(hit, dest_groups[i], dest_group)
-                    key = jnp.where(hit, order_ref[i] + 1, key)
+                    key = jnp.where(hit, small_ref[0, tiles_here + i] + 1, key)
                 first_table[slot] = tile
                 limit_table[slot] = limit
                 row = jnp.where(lane == p, dest_group, row)
@@ -179,8 +179,12 @@
             g_copy(c, k, px, py, group).start()
         own_copy(c).start()
 
-    gain_copy = pltpu.make_async_copy(gain_ref, gain, gain_sem)
-    gain_copy.start()
+    small = [
+        pltpu.make_async_copy(small_in, small_ref, small_sem),
+        pltpu.make_async_copy(gain_ref, gain, gain_sem),
+    ]
+    for copy in small:
+        copy.start()
     for c in range(chunks):
         load(c).start()
     barrier = pltpu.get_barrier_semaphore()
@@ -191,8 +195,9 @@
     for k in range(groups - 1):
         px, py = peer_of(k)
         pl.semaphore_signal(barrier, inc=1, device_id=(px, py, gz), device_id_type=MESH)
+    for copy in small:
+        copy.wait()
     fill_tables()
-    gain_copy.wait()
     prepare(0)
     pl.semaphore_wait(barrier, depth - 1 + groups - 1)
     for dz in range(1, depth):
@@ -227,30 +232,20 @@
         own_copy(c).wait()
 
 
-def place_kernel(source_ref, filled_ref, blocks_ref, out_ref, held, zeros, in_sem, out_sem):
+def place_kernel(source_ref, filled_ref, blocks_ref, out_ref, zeros, out_sem):
     cap = out_ref.shape[0]
 
-    def fetch(slot):
-        return pltpu.make_async_copy(blocks_ref.at[source_ref[slot]], held.at[slot], in_sem.at[slot])
-
     def store(slot):
-        return pltpu.make_async_copy(held.at[slot], out_ref.at[slot], out_sem.at[slot])
+        return pltpu.make_async_copy(blocks_ref.at[source_ref[slot]], out_ref.at[slot], out_sem.at[slot])
 
     for slot in range(cap):
-        pl.when(filled_ref[slot] == 1)(lambda slot=slot: fetch(slot).start())
+        pl.when(filled_ref[slot] == 1)(lambda slot=slot: store(slot).start())
     zeros[...] = jnp.zeros_like(zeros)
     for slot in range(cap):
 
         @pl.when(filled_ref[slot] == 0)
         def _():
             pltpu.make_async_copy(zeros, out_ref.at[slot], out_sem.at[slot]).start()
-
-    for slot in range(cap):
-
-        @pl.when(filled_ref[slot] == 1)
-        def _():
-            fetch(slot).wait()
-            store(slot).start()
 
     for slot in range(cap):
         store(slot).wait()
@@ -271,16 +266,20 @@
     vmem = pl.BlockSpec(memory_space=pltpu.VMEM)
     hbm = pl.BlockSpec(memory_space=pl.ANY)
     lanes = -(-2 * per_peer // 128) * 128
+    small = jnp.concatenate([dest_device, shuffle_key, lengths])
+    small = jnp.pad(small, (0, -small.shape[0] % 128))[None, :]
     received, key_rows = pl.pallas_call(
         functools.partial(exchange_kernel, (nx, ny, depth, per_peer, chunk_rows)),
         out_shape=(
             jax.ShapeDtypeStruct((groups, tile_rows, width), jnp.bfloat16),
             jax.ShapeDtypeStruct((groups, 1, 128), jnp.int32),
         ),
-        in_specs=[smem, smem, smem, hbm, hbm],
+        in_specs=[hbm] * 3,
         out_specs=(hbm, vmem),
         scratch_shapes=[
+            pltpu.SMEM(small.shape, jnp.int32),
             pltpu.VMEM((1, width), jnp.float32),
+            pltpu.SemaphoreType.DMA,
             pltpu.SMEM((slots,), jnp.int32),
             pltpu.SMEM((slots,), jnp.int32),
             pltpu.VMEM((depth, 1, lanes), jnp.int32),
@@ -306,10 +305,10 @@
         + [pltpu.VMEM((slots, rows, width), jnp.bfloat16) for rows in chunk_rows]
         + [pltpu.VMEM((groups, rows, width), jnp.bfloat16) for rows in chunk_rows],
         compiler_params=pltpu.CompilerParams(
-            collective_id=0, has_side_effects=True, vmem_limit_bytes=52 * 1024 * 1024
+            collective_id=0, has_side_effects=True, vmem_limit_bytes=36 * 1024 * 1024
         ),
         name="exchange",
-    )(dest_device, shuffle_key, lengths, embeds, gain.reshape(1, width))
+    )(small, embeds, gain.reshape(1, width))
 
     key_of = key_rows[:, 0, 0]
     valid = key_of > 0
@@ -322,15 +321,13 @@
     return pl.pallas_call(
         place_kernel,
         out_shape=jax.ShapeDtypeStruct((cap, tile_rows, width), jnp.bfloat16),
-        in_specs=[smem, smem, hbm],
+        in_specs=[smem, smem, vmem],
         out_specs=hbm,
         scratch_shapes=[
-            pltpu.VMEM((cap, tile_rows, width), jnp.bfloat16),
             pltpu.VMEM((tile_rows, width), jnp.bfloat16),
             pltpu.SemaphoreType.DMA((cap,)),
-            pltpu.SemaphoreType.DMA((cap,)),
         ],
-        compiler_params=pltpu.CompilerParams(vmem_limit_bytes=52 * 1024 * 1024),
+        compiler_params=pltpu.CompilerParams(vmem_limit_bytes=24 * 1024 * 1024),
         name="place",
     )(source, filled, received)
 

time: 204 us -> 201 us (0.985)
  Pallas kernels: 200 us -> 197 us
    pallas_call x1, Pallas kernels: 6.64 us -> 3.96 us  [shards(): pl.pallas_call(place_kernel, out_shape=jax.ShapeDtypeStruct((cap, tile_ro...]
where the time goes in v5:
time: 201 us
  Pallas kernels  197 us (98%)
  local copies, waits for them, and re-layouts  3.27 us (2%)
    pallas_call x1, Pallas kernels, shards(): pl.pallas_call(functools.partial(exchange_kernel, (nx, ny, depth, per_pee...  193 us

profile of v5, /device:TPU:9, one launch (start us, length us, event | category | flops | bytes accessed | tf_op | source)
XLA Modules:
  0.0 201.1 jit_solution(12787704376812360420)
XLA Ops:
  0.0 0.8 pad_add_fusion
  0.8 0.0 copy-start
  0.8 2.2 %copy-done = bf16[8,128,2048]{2,1,0:T(8,128)(2,1)S(1)} copy-done((bf16[8,128,2048]{2,1,0:T(8,128)(2,1)S(1)}, bf16[8,128,2048]{2,1,0:T(8,128)(2,1)}, u32[]{:S(2)}) %copy-start) | copy-done | bytes 4194328
  3.0 0.0 copy-start.1
  3.0 0.7 copy-done.1
  3.7 192.8 %exchange.1 = (bf16[16,128,2048]{2,1,0:T(8,128)(2,1)S(1)}, s32[16,1,128]{2,1,0:T(1,128)S(1)}) custom-call(s32[1,128]{1,0:T(1,128)S(1)} %pad_bitcast_fusion.small_in, bf16[8,128,2048]{2,1,0:T(8,128)(2,1)S(1)} %copy-done, f32[1,2048]{1,0:T(1,128)S(1)} %bitcast.3), custom_call_target="tpu_custom_call" | custom-call | tf_op jit(solution)/shard_map/exchange/pallas_call | solution.py:271
  196.5 0.4 slice_reduce_fusion
  196.9 0.2 convert_reduce_fusion.1
  197.1 0.1 convert_reduce_fusion
  197.2 4.0 %place.1 = bf16[16,128,2048]{2,1,0:T(8,128)(2,1)} custom-call(s32[16]{0:T(128)S(1)} %get-tuple-element.10.source_ref, s32[16]{0:T(128)S(1)} %get-tuple-element.9.filled_ref, bf16[16,128,2048]{2,1,0:T(8,128)(2,1)S(1)} %get-tuple-element.8.blocks_ref), custom_call_target="tpu_custom_call" | custom-call | tf_op jit(solution)/shard_map/place/pallas_call | solution.py:321
  (2 shorter events, 0.0 us)
Async XLA Ops:
  0.8 2.2 %copy-start = (bf16[8,128,2048]{2,1,0:T(8,128)(2,1)S(1)}, bf16[8,128,2048]{2,1,0:T(8,128)(2,1)}, u32[]{:S(2)}) copy-start(bf16[8,128,2048]{2,1,0:T(8,128)(2,1)} %x_ref.1) | copy-start | bytes 12582916
  3.0 0.7 copy-start.1
